TPU v7x, 32 devices: a whole 2x2x4 slice. The times are simulated.
32 devices in a mesh: rows: 8 (over z, y), cols: 4 (over x, core).
Axes of the slice: x: 2, y: 2, z: 4, core: 2. Of those that a mesh axis runs over, the one named last changes fastest.
Arguments:
- factor_a: bfloat16 [16384, 48, 48], P('rows'), may hold values from -0.875 to 0.875
- factor_b: bfloat16 [16384, 48, 48], P('rows'), may hold values from -0.046875 to 0.046875
- next_factor: bfloat16 [16384, 48, 48], P(('rows', 'cols')), may hold values from -6 to 6
- sketch_leg: bfloat16 [48, 32], replicated, may hold values from -6 to 6
- sketch_rows: bfloat16 [16384, 32], P('rows', 'cols'), may hold values from -6 to 6
Outputs:
- basis: float32 [32, 16384, 48], P(None, ('rows', 'cols'))
- squeezed: float32 [32, 48], replicated
All inputs are finite; a program needn't handle non-finite values.
Results may differ from a plain program's by a relative error of at most 0.0003.
Values sent between devices are 32-bit elements; how exact they have to be, the bound alone decides.
No kernel may reach another device: no remote copies, remote signals or barrier semaphores. Data moves between devices by JAX's collectives and lax.ppermute only.
A program may use at most 128 MiB of HBM per device.

v0:
```python
import jax
import jax.numpy as jnp
from jax import lax
from jax.sharding import PartitionSpec as P


def per_device(factor_a, factor_b, next_factor, sketch_leg, sketch_rows):
    high = lax.Precision.HIGHEST
    local_rows = factor_a.shape[0]
    width = factor_a.shape[1]
    col_parts = lax.axis_size("cols")
    quarter = local_rows // col_parts
    col_index = lax.axis_index("cols")
    count = local_rows * lax.axis_size("rows") * width
    start = col_index * quarter
    far_part = jnp.einsum("sp,syk->pyk", sketch_rows, factor_b, preferred_element_type=jnp.float32)
    far = lax.psum(far_part, "rows")
    far_all = lax.all_gather(far, "cols", axis=0, tiled=True)
    own_rows = lax.dynamic_slice_in_dim(factor_a, start, quarter, 0)
    near = jnp.einsum("sxk,xp->psk", own_rows, sketch_leg, preferred_element_type=jnp.float32)
    sketch = jnp.einsum("psk,pyk->psy", near, far_all, precision=high)
    columns = sketch.shape[0]
    flat = sketch.reshape(columns, quarter * width)
    own_next = next_factor.reshape(quarter * width, width).astype(jnp.float32)
    gram_part = jnp.dot(flat, flat.T, precision=high)
    root_count = jnp.sqrt(jnp.float32(count))
    gram = lax.psum(gram_part, ("rows", "cols")) / count
    lower = jnp.linalg.cholesky(gram)
    basis = jax.scipy.linalg.solve_triangular(lower, flat, lower=True)
    squeeze_part = jnp.dot(basis, own_next, precision=high)
    squeezed = lax.psum(squeeze_part, ("rows", "cols")) / root_count
    return (basis.reshape(columns, quarter, width), squeezed)


def solution(mesh):
    return jax.shard_map(
        per_device,
        mesh=mesh,
        in_specs=(
            P("rows", None, None),
            P("rows", None, None),
            P(("rows", "cols"), None, None),
            P(),
            P("rows", "cols"),
        ),
        out_specs=(P(None, ("rows", "cols"), None), P()),
        check_vma=False,
    )
```

profile of v0, /device:TPU:0, one launch (start us, length us, event | category | flops | bytes accessed | tf_op | source)
XLA Modules:
  0.0 238.8 jit_solution(5856863479625042245)
XLA Ops:
  7.2 0.7 copy-done
  7.9 8.9 %fusion.12 = f32[8,48,48]{2,0,1:T(8,128)} fusion(bf16[2048,48,48]{0,2,1:T(8,128)(2,1)} %param.6, bf16[2048,8]{0,1:T(8,128)(2,1)S(1)} %copy-done), kind=kOutput, calls=%fused_computation.8 | convolution fusion | flops 75497472 | bytes 9543680 | tf_op jit(solution)/shard_map/sp,syk->pyk/dot_general | solution.py:16
  16.9 1.8 constant_dynamic-slice_fusion
  18.7 3.4 %fusion.6 = f32[32,512,48]{1,0,2:T(8,128)} fusion(bf16[512,48,48]{0,2,1:T(8,128)(2,1)S(1)} %constant_dynamic-slice_fusion, bf16[48,32]{0,1:T(8,128)(2,1)S(1)} %copy-done.2), kind=kOutput, calls=%fused_computation.6 | convolution fusion | flops 75497472 | bytes 5508096 | tf_op jit(solution)/shard_map/sxk,xp->psk/dot_general | solution.py:20
  22.1 5.0 %copy.27 = bf16[512,48,48]{1,0,2:T(8,128)(2,1)} copy(bf16[512,48,48]{0,2,1:T(8,128)(2,1)S(1)} %copy-done.1) | data formatting | bytes 4718592 | tf_op args[2]
  27.2 14.0 %reshape.25 = bf16[24576,48]{0,1:T(8,128)(2,1)} reshape(bf16[512,48,48]{1,0,2:T(8,128)(2,1)} %copy.27) | data formatting | bytes 4718592 | tf_op jit(solution)/shard_map/reshape | solution.py:24
  41.1 49.3 %all-reduce.2.cloned.1.call-done = f32[8,48,48]{2,0,1:T(8,128)} async-done(((f32[8,48,48]{2,0,1:T(8,128)}), f32[8,48,48]{2,0,1:T(8,128)}) %all-reduce.2.cloned.1.call-update) | async-done | bytes 73744 | tf_op jit(solution)/shard_map/psum | solution.py:17
  90.4 1.0 copy.20
  91.4 8.8 %all_gather.3 = f32[32,48,48]{2,1,0:T(8,128)S(1)} all-gather(f32[8,48,48]{2,1,0:T(8,128)S(1)} %copy.20), channel_id=1, replica_groups=mesh['rows'=8,'cols'=4] {'cols'}, dimensions={0}, use_global_device_ids=true | all-gather | bytes 368640 | tf_op jit(solution)/shard_map/all_gather | solution.py:18
  100.1 6.7 %fusion.2 = f32[32,512,48]{1,2,0:T(8,128)S(1)} fusion(f32[32,48,48]{2,1,0:T(8,128)S(1)} %all_gather.3, f32[32,512,48]{1,0,2:T(8,128)} %fusion.6), kind=kOutput, calls=%fused_computation.2 | convolution fusion | flops 452984832 | bytes 6586368 | tf_op jit(solution)/shard_map/psk,pyk->psy/dot_general | solution.py:21
  106.9 4.2 %fusion.9 = f32[32,32]{0,1:T(8,128)S(1)} fusion(f32[32,512,48]{1,2,0:T(8,128)S(1)} %fusion.2), kind=kOutput, calls=%fused_computation.7 | convolution fusion | flops 301989888 | bytes 3149824 | tf_op jit(solution)/shard_map/dot_general | solution.py:25
  111.1 4.7 %copy.26 = f32[32,512,48]{2,1,0:T(8,128)} copy(f32[32,512,48]{1,2,0:T(8,128)S(1)} %fusion.2) | data formatting | bytes 6291456 | tf_op jit(solution)/shard_map/psk,pyk->psy/dot_general | solution.py:21
  115.8 38.7 %psum.22 = f32[32,32]{0,1:T(8,128)S(1)} all-reduce(f32[32,32]{0,1:T(8,128)S(1)} %fusion.9), channel_id=1, replica_groups=mesh['rows'=8,'cols'=4] {'rows','cols'}, use_global_device_ids=true, to_apply=%region_1.0 | all-reduce | flops 1024 | bytes 8192 | tf_op jit(solution)/shard_map/psum | solution.py:27
  154.5 2.9 %cholesky.16 = f32[32,32]{1,0:T(8,128)S(1)} custom-call(f32[32,32]{1,0:T(8,128)S(1)} %fusion.17), custom_call_target="Cholesky" | custom-call | tf_op jit(solution)/shard_map/jit(cholesky)/cholesky | solution.py:28
  157.5 0.6 compare_reduce_fusion
  158.1 0.7 fusion.14
  158.8 2.4 %custom-call.7 = f32[1,32,32]{1,2,0:T(8,128)S(1)} custom-call(f32[1,32,32]{2,1,0:T(8,128)S(1)} %fusion.14), custom_call_target="InvertDiagBlocksLowerTriangular" | custom-call | tf_op jit(solution)/shard_map/jit(_solve_triangular)/triangular_solve | solution.py:29
  161.2 9.8 %reshape.23 = f32[32,24576]{1,0:T(8,128)} reshape(f32[32,512,48]{2,1,0:T(8,128)} %copy.26) | data formatting | bytes 6291456 | tf_op jit(solution)/shard_map/reshape | solution.py:23
  171.0 4.6 %fusion.15 = f32[32,24576]{1,0:T(8,128)S(1)} fusion(f32[32,24576]{1,0:T(8,128)} %reshape.23, f32[1,32,32]{1,2,0:T(8,128)S(1)} %custom-call.7), kind=kOutput, calls=%fused_computation.12 | convolution fusion | flops 301989888 | bytes 6295552 | tf_op jit(solution)/shard_map/jit(_solve_triangular)/triangular_solve | solution.py:29
  175.6 5.4 %reshape.24 = f32[32,512,48]{2,1,0:T(8,128)} reshape(f32[32,24576]{1,0:T(8,128)S(1)} %fusion.15) | data formatting | bytes 6291456 | tf_op jit(solution)/shard_map/reshape | solution.py:32
  181.0 3.7 %fusion.19 = f32[32,48]{1,0:T(8,128)S(1)} fusion(f32[32,24576]{1,0:T(8,128)S(1)} %fusion.15, bf16[24576,48]{0,1:T(8,128)(2,1)} %reshape.25), kind=kOutput, calls=%fused_computation.24 | convolution fusion | flops 452984832 | bytes 5511168 | tf_op jit(solution)/shard_map/dot_general | solution.py:30
  184.7 40.1 %psum.23 = f32[32,48]{1,0:T(8,128)S(1)} all-reduce(f32[32,48]{1,0:T(8,128)S(1)} %fusion.19), channel_id=1, replica_groups=mesh['rows'=8,'cols'=4] {'rows','cols'}, use_global_device_ids=true, to_apply=%region_4.5 | all-reduce | flops 1536 | bytes 12288 | tf_op jit(solution)/shard_map/psum | solution.py:31
  224.8 0.6 broadcast_multiply_fusion
  225.5 6.5 %copy.28 = f32[32,512,48]{1,2,0:T(8,128)} copy(f32[32,512,48]{2,1,0:T(8,128)} %reshape.24) | data formatting | bytes 6291456
  (11 shorter events, 0.2 us)
Async XLA Ops:
  7.2 0.8 copy-start
  7.2 83.2 %all-reduce.2.cloned.1.call-start = ((), (), s32[]{:S(2)}) async-start(), calls=%async_computation | async-start | bytes 393216 | tf_op jit(solution)/shard_map/psum | solution.py:17
  16.8 1.9 copy-start.2
  18.7 3.4 %copy-start.1 = (bf16[512,48,48]{0,2,1:T(8,128)(2,1)S(1)}, bf16[512,48,48]{0,2,1:T(8,128)(2,1)}, u32[]{:S(2)}) copy-start(bf16[512,48,48]{0,2,1:T(8,128)(2,1)} %param.7) | copy-start | bytes 7077892
Sparse Core Ops, SparseCore 0:
  17.0 73.3 all-reduce.1
where the time goes:
time: 239 us
  blocking collectives  87.6 us (37%)
  waiting for transfers between devices  49.3 us (21%)
  local copies, waits for them, and re-layouts  48.9 us (20%)
  matrix products  31.5 us (13%)
  between operations  14.1 us (6%)
  other arithmetic  7.3 us (3%)
    psum x1, waiting for transfers between devices, per_device(): far = lax.psum(far_part, 'rows')  49.3 us
    psum x1, blocking collectives, per_device(): squeezed = lax.psum(squeeze_part, ('rows', 'cols')) / root_count  40.1 us
    psum x1, blocking collectives, per_device(): gram = lax.psum(gram_part, ('rows', 'cols')) / count  38.7 us
    reshape x1, local copies, waits for them, and re-layouts, per_device(): own_next = next_factor.reshape(quarter * width, width).astype(jnp.float32)  14 us
    unnamed x8, local copies, waits for them, and re-layouts  12.3 us
    reshape x1, local copies, waits for them, and re-layouts, per_device(): flat = sketch.reshape(columns, quarter * width)  9.77 us
    dot_general x1, matrix products, per_device(): jnp.einsum('sp,syk->pyk', sketch_rows, factor_b, preferred_element_type=j...  8.91 us
    all_gather x1, blocking collectives, per_device(): far_all = lax.all_gather(far, 'cols', axis=0, tiled=True)  8.76 us
  transfers between devices with their start and end apart: 1, of which 1 were waited for; matrix products, arithmetic and copies ran while one was open for 10% of the time, Pallas kernels for 0%

commit v1 on v0

--- a/solution.py
+++ b/solution.py
@@ -14,7 +14,8 @@
     count = local_rows * lax.axis_size("rows") * width
     start = col_index * quarter
     far_part = jnp.einsum("sp,syk->pyk", sketch_rows, factor_b, preferred_element_type=jnp.float32)
-    far = lax.psum(far_part, "rows")
+    parts = lax.all_gather(far_part, "rows")
+    far = jnp.sum(parts, axis=0)
     far_all = lax.all_gather(far, "cols", axis=0, tiled=True)
     own_rows = lax.dynamic_slice_in_dim(factor_a, start, quarter, 0)
     near = jnp.einsum("sxk,xp->psk", own_rows, sketch_leg, preferred_element_type=jnp.float32)

time: 239 us -> 211 us (0.88)
  waiting for transfers between devices: 49.3 us -> 0 us
  blocking collectives: 87.6 us -> 126 us
  between operations: 14.1 us -> 0.73 us
  matrix products: 31.5 us -> 26.1 us
    psum x1 -> x0, waiting for transfers between devices: 49.3 us -> none  [per_device(): far = lax.psum(far_part, 'rows')]
    all_gather x0 -> x1, blocking collectives: none -> 38.7 us  [per_device(): parts = lax.all_gather(far_part, 'rows')]
  transfers between devices with their start and end apart: 1 -> 0, of which waited for: 1 -> 0; matrix products, arithmetic and copies ran while one was open for 10% -> 0% of each run, Pallas kernels for 0% -> 0%
where the time goes in v1:
time: 211 us; the launch traced here: 210 us
  blocking collectives  126 us (60%)
  local copies, waits for them, and re-layouts  49.8 us (24%)
  matrix products  26.1 us (12%)
  other arithmetic  7.47 us (4%)
    psum x1, blocking collectives, per_device(): squeezed = lax.psum(squeeze_part, ('rows', 'cols')) / root_count  41 us
    all_gather x1, blocking collectives, per_device(): parts = lax.all_gather(far_part, 'rows')  38.7 us
    psum x1, blocking collectives, per_device(): gram = lax.psum(gram_part, ('rows', 'cols')) / count  37.8 us
    unnamed x8, local copies, waits for them, and re-layouts  14.1 us
    reshape x1, local copies, waits for them, and re-layouts, per_device(): own_next = next_factor.reshape(quarter * width, width).astype(jnp.float32)  13.9 us
    reshape x1, local copies, waits for them, and re-layouts, per_device(): flat = sketch.reshape(columns, quarter * width)  9.74 us
    all_gather x1, blocking collectives, per_device(): far_all = lax.all_gather(far, 'cols', axis=0, tiled=True)  8.6 us
    dot_general x1, matrix products, per_device(): jnp.einsum('sp,syk->pyk', sketch_rows, factor_b, preferred_element_type=j...  7 us

profile of v1, /device:TPU:0, one launch (start us, length us, event | category | flops | bytes accessed | tf_op | source)
XLA Modules:
  0.0 210.2 jit_solution(11933045794093815620)
XLA Ops:
  0.7 0.7 copy-done
  1.4 7.0 %fusion.12 = f32[8,48,48]{2,0,1:T(8,128)S(1)} fusion(bf16[2048,48,48]{0,2,1:T(8,128)(2,1)} %param.6, bf16[2048,8]{0,1:T(8,128)(2,1)S(1)} %copy-done), kind=kOutput, calls=%fused_computation.9 | convolution fusion | flops 75497472 | bytes 9543680 | tf_op jit(solution)/shard_map/sp,syk->pyk/dot_general | solution.py:16
  8.4 38.7 %all-gather = f32[64,48,48]{2,0,1:T(8,128)S(1)} all-gather(f32[8,48,48]{2,0,1:T(8,128)S(1)} %fusion.12), channel_id=2, replica_groups=mesh['rows'=8,'cols'=4] {'rows'}, dimensions={0}, use_global_device_ids=true | all-gather | bytes 663552 | tf_op jit(solution)/shard_map/all_gather | solution.py:17
  47.1 0.2 bitcast_reduce_fusion
  47.4 8.6 %all_gather.11 = f32[32,48,48]{2,1,0:T(8,128)S(1)} all-gather(f32[8,48,48]{2,1,0:T(8,128)S(1)} %copy.20), channel_id=1, replica_groups=mesh['rows'=8,'cols'=4] {'cols'}, dimensions={0}, use_global_device_ids=true | all-gather | bytes 368640 | tf_op jit(solution)/shard_map/all_gather | solution.py:19
  56.0 1.8 constant_dynamic-slice_fusion
  57.8 1.7 fusion.6
  59.5 4.9 %fusion.2 = f32[32,512,48]{1,2,0:T(8,128)S(1)} fusion(f32[32,48,48]{2,1,0:T(8,128)S(1)} %all_gather.11, f32[32,512,48]{1,0,2:T(8,128)S(1)} %fusion.6), kind=kOutput, calls=%fused_computation.2 | convolution fusion | flops 452984832 | bytes 6586368 | tf_op jit(solution)/shard_map/psk,pyk->psy/dot_general | solution.py:22
  64.4 4.2 %fusion.9 = f32[32,32]{0,1:T(8,128)S(1)} fusion(f32[32,512,48]{1,2,0:T(8,128)S(1)} %fusion.2), kind=kOutput, calls=%fused_computation.8 | convolution fusion | flops 301989888 | bytes 3149824 | tf_op jit(solution)/shard_map/dot_general | solution.py:26
  68.6 37.8 %psum.14 = f32[32,32]{0,1:T(8,128)S(1)} all-reduce(f32[32,32]{0,1:T(8,128)S(1)} %fusion.9), channel_id=1, replica_groups=mesh['rows'=8,'cols'=4] {'rows','cols'}, use_global_device_ids=true, to_apply=%region_1.0 | all-reduce | flops 1024 | bytes 8192 | tf_op jit(solution)/shard_map/psum | solution.py:28
  106.5 2.9 %cholesky.16 = f32[32,32]{1,0:T(8,128)S(1)} custom-call(f32[32,32]{1,0:T(8,128)S(1)} %fusion.17), custom_call_target="Cholesky" | custom-call | tf_op jit(solution)/shard_map/jit(cholesky)/cholesky | solution.py:29
  109.4 0.6 compare_reduce_fusion
  110.1 0.7 fusion.14
  110.7 2.4 %custom-call.7 = f32[1,32,32]{1,2,0:T(8,128)S(1)} custom-call(f32[1,32,32]{2,1,0:T(8,128)S(1)} %fusion.14), custom_call_target="InvertDiagBlocksLowerTriangular" | custom-call | tf_op jit(solution)/shard_map/jit(_solve_triangular)/triangular_solve | solution.py:30
  113.2 4.7 %copy.26 = f32[32,512,48]{2,1,0:T(8,128)} copy(f32[32,512,48]{1,2,0:T(8,128)S(1)} %fusion.2) | data formatting | bytes 6291456 | tf_op jit(solution)/shard_map/psk,pyk->psy/dot_general | solution.py:22
  117.9 9.7 %reshape.23 = f32[32,24576]{1,0:T(8,128)} reshape(f32[32,512,48]{2,1,0:T(8,128)} %copy.26) | data formatting | bytes 6291456 | tf_op jit(solution)/shard_map/reshape | solution.py:24
  127.7 4.6 %fusion.15 = f32[32,24576]{1,0:T(8,128)S(1)} fusion(f32[32,24576]{1,0:T(8,128)} %reshape.23, f32[1,32,32]{1,2,0:T(8,128)S(1)} %custom-call.7), kind=kOutput, calls=%fused_computation.13 | convolution fusion | flops 301989888 | bytes 6295552 | tf_op jit(solution)/shard_map/jit(_solve_triangular)/triangular_solve | solution.py:30
  132.3 6.8 %copy.27 = bf16[512,48,48]{1,0,2:T(8,128)(2,1)} copy(bf16[512,48,48]{0,2,1:T(8,128)(2,1)} %param.7) | data formatting | bytes 4718592 | tf_op args[2]
  139.1 13.9 %reshape.25 = bf16[24576,48]{0,1:T(8,128)(2,1)} reshape(bf16[512,48,48]{1,0,2:T(8,128)(2,1)} %copy.27) | data formatting | bytes 4718592 | tf_op jit(solution)/shard_map/reshape | solution.py:25
  153.1 3.7 %fusion.19 = f32[32,48]{1,0:T(8,128)S(1)} fusion(f32[32,24576]{1,0:T(8,128)S(1)} %fusion.15, bf16[24576,48]{0,1:T(8,128)(2,1)} %reshape.25), kind=kOutput, calls=%fused_computation.25 | convolution fusion | flops 452984832 | bytes 5511168 | tf_op jit(solution)/shard_map/dot_general | solution.py:31
  156.7 41.0 %psum.15 = f32[32,48]{1,0:T(8,128)S(1)} all-reduce(f32[32,48]{1,0:T(8,128)S(1)} %fusion.19), channel_id=1, replica_groups=mesh['rows'=8,'cols'=4] {'rows','cols'}, use_global_device_ids=true, to_apply=%region_4.5 | all-reduce | flops 1536 | bytes 12288 | tf_op jit(solution)/shard_map/psum | solution.py:32
  197.7 0.6 broadcast_multiply_fusion
  198.3 5.4 %reshape.24 = f32[32,512,48]{2,1,0:T(8,128)} reshape(f32[32,24576]{1,0:T(8,128)S(1)} %fusion.15) | data formatting | bytes 6291456 | tf_op jit(solution)/shard_map/reshape | solution.py:33
  203.7 6.5 %copy.28 = f32[32,512,48]{1,2,0:T(8,128)} copy(f32[32,512,48]{2,1,0:T(8,128)} %reshape.24) | data formatting | bytes 6291456
  (10 shorter events, 0.2 us)
Async XLA Ops:
  0.6 0.8 copy-start
  47.3 10.5 %copy-start.2 = (bf16[48,32]{0,1:T(8,128)(2,1)S(1)}, bf16[48,32]{0,1:T(8,128)(2,1)}, u32[]{:S(2)}) copy-start(bf16[48,32]{0,1:T(8,128)(2,1)} %param.8) | copy-start | bytes 9220
  198.3 11.9 %copy-start.1 = (bf16[2048,8]{0,1:T(8,128)(2,1)S(1)}, bf16[2048,8]{0,1:T(8,128)(2,1)}, u32[]{:S(2)}) copy-start(bf16[2048,8]{0,1:T(8,128)(2,1)} %param.9) | copy-start | bytes 98308
